TPU v7x, 128 devices: a whole 4x4x4 slice. The times are simulated.
128 devices in a mesh: data: 1, cp: 64 (over z, y, x), tp: 2 (over core).
Axes of the slice: x: 4, y: 4, z: 4, core: 2. Of those that a mesh axis runs over, the one named last changes fastest.
Arguments:
- act_in: bfloat16 [2, 8192, 2048], P(None, ('data', 'cp', 'tp'))
- route_ids: int32 [2, 8192, 2], P(None, ('data', 'cp', 'tp'))
- route_gates: float32 [2, 8192, 2], P(None, ('data', 'cp', 'tp'))
- w_query: bfloat16 [2048, 32, 128], P(None, 'tp')
- w_key: bfloat16 [2048, 4, 128], P(None, 'tp')
- w_value: bfloat16 [2048, 4, 128], P(None, 'tp')
- w_out: bfloat16 [32, 128, 2048], P('tp')
- w_gate: bfloat16 [128, 2048, 768], P(('cp', 'tp'))
- w_up: bfloat16 [128, 2048, 768], P(('cp', 'tp'))
- w_down: bfloat16 [128, 768, 2048], P(('cp', 'tp'))
Outputs:
- output: bfloat16 [2, 8192, 2048], P(None, ('data', 'cp', 'tp'))
All inputs are finite; a program needn't handle non-finite values.
Results may differ from a plain program's by a relative error of at most 0.00548.
Values are sent between devices in bfloat16 or wider.
A program may use at most 1 GiB of HBM per device.

v0:
```python
import jax
import jax.numpy as jnp
from jax import lax
from jax.sharding import PartitionSpec as P


def pick_rows(row_table, row_ids):
    return jnp.take(row_table, row_ids, axis=0, mode='fill', fill_value=0)


def attend_local(act_in, w_query, w_key, w_value, w_out, cp_size, tp_size):
    n_micro, tokens, hidden = act_in.shape
    q_local, head_dim = w_query.shape[1], w_query.shape[2]
    kv_local = w_key.shape[1]
    group_size = q_local // kv_local
    half_rows = tokens * tp_size
    piece_len = half_rows // 2
    seq_len = half_rows * cp_size
    cp_rank = lax.axis_index('cp')
    x_half = lax.all_gather(act_in, 'tp', axis=1, tiled=True)
    query_rows = jnp.einsum('bsh,hnd->bsnd', x_half, w_query, preferred_element_type=jnp.float32).astype(jnp.bfloat16)
    query_rows = query_rows.reshape(n_micro, half_rows, kv_local, group_size, head_dim)
    key_half = jnp.einsum('bsh,hnd->bsnd', x_half, w_key, preferred_element_type=jnp.float32).astype(jnp.bfloat16)
    value_half = jnp.einsum('bsh,hnd->bsnd', x_half, w_value, preferred_element_type=jnp.float32).astype(jnp.bfloat16)
    key_all = lax.all_gather(key_half, 'cp', axis=1, tiled=True)
    value_all = lax.all_gather(value_half, 'cp', axis=1, tiled=True)
    local_ix = jnp.arange(half_rows)
    owner_ix = jnp.arange(cp_size)[:, None]
    key_pos = jnp.where(local_ix < piece_len, owner_ix * piece_len + local_ix, (2 * cp_size - 1 - owner_ix) * piece_len + local_ix - piece_len).reshape(seq_len)
    score_scale = head_dim ** -0.5
    halves = []
    for half_id in range(2):
        piece_id = cp_rank if half_id == 0 else 2 * cp_size - 1 - cp_rank
        query_pos = piece_id * piece_len + jnp.arange(piece_len)
        q_part = query_rows[:, half_id * piece_len:(half_id + 1) * piece_len]
        scores = jnp.einsum('bqhgd,bkhd->bhgqk', q_part, key_all, preferred_element_type=jnp.float32) * score_scale
        scores = jnp.where(key_pos[None, :] <= query_pos[:, None], scores, -jnp.inf)
        row_peak = jnp.max(scores, axis=-1, keepdims=True)
        exp_scores = jnp.exp(scores - row_peak)
        row_sum = jnp.sum(exp_scores, axis=-1)
        weighted = jnp.einsum('bhgqk,bkhd->bqhgd', exp_scores.astype(jnp.bfloat16), value_all, preferred_element_type=jnp.float32)
        weighted = weighted / jnp.transpose(row_sum, (0, 3, 1, 2))[..., None]
        halves.append(weighted.astype(jnp.bfloat16))
    attn_rows = jnp.concatenate(halves, axis=1).reshape(n_micro, half_rows, q_local, head_dim)
    partial = jnp.einsum('bsnd,ndh->bsh', attn_rows, w_out, preferred_element_type=jnp.float32)
    attn_sum = lax.psum_scatter(partial, 'tp', scatter_dimension=1, tiled=True)
    return (act_in.astype(jnp.float32) + attn_sum).astype(jnp.bfloat16)


def dispatch_experts(mid_rows, route_ids, route_gates, w_gate, w_up, w_down, experts):
    n_micro, tokens, hidden = mid_rows.shape
    capacity = (4 * tokens) // experts
    flat_ids = route_ids.reshape(n_micro, 2 * tokens)
    expert_hits = (flat_ids[..., None] == jnp.arange(experts)).astype(jnp.int32)
    slot_rank = jnp.sum((jnp.cumsum(expert_hits, axis=1) - 1) * expert_hits, axis=-1)
    dest_slot = flat_ids * capacity + slot_rank
    micro_ix = jnp.arange(n_micro)[:, None]
    token_of = jnp.broadcast_to((jnp.arange(2 * tokens, dtype=jnp.int32) // 2)[None, :], dest_slot.shape)
    source_row = jnp.full((n_micro, experts * capacity), tokens, jnp.int32).at[micro_ix, dest_slot].set(token_of)
    send_buf = jax.vmap(pick_rows)(mid_rows, source_row).reshape(n_micro, experts, capacity, hidden)
    recv_buf = lax.all_to_all(send_buf, ('cp', 'tp'), 1, 1, tiled=True)
    expert_in = recv_buf.reshape(n_micro, experts * capacity, hidden)
    gate_act = jnp.einsum('bth,hf->btf', expert_in, w_gate[0], preferred_element_type=jnp.float32)
    up_act = jnp.einsum('bth,hf->btf', expert_in, w_up[0], preferred_element_type=jnp.float32)
    mixed_act = (jax.nn.silu(gate_act) * up_act).astype(jnp.bfloat16)
    expert_out = jnp.einsum('btf,fh->bth', mixed_act, w_down[0], preferred_element_type=jnp.float32).astype(jnp.bfloat16)
    back_buf = lax.all_to_all(expert_out.reshape(n_micro, experts, capacity, hidden), ('cp', 'tp'), 1, 1, tiled=True)
    picked = jax.vmap(pick_rows)(back_buf.reshape(n_micro, experts * capacity, hidden), dest_slot).reshape(n_micro, tokens, 2, hidden)
    combined = route_gates[:, :, 0:1] * picked[:, :, 0].astype(jnp.float32) + route_gates[:, :, 1:2] * picked[:, :, 1].astype(jnp.float32)
    return (mid_rows.astype(jnp.float32) + combined).astype(jnp.bfloat16)


def solution(mesh):
    cp_size = mesh.shape['cp']
    tp_size = mesh.shape['tp']
    experts = cp_size * tp_size
    row_spec = P(None, ('data', 'cp', 'tp'), None)
    head_spec = P(None, 'tp', None)
    out_spec = P('tp', None, None)
    expert_spec = P(('cp', 'tp'), None, None)

    def device_step(act_in, route_ids, route_gates, w_query, w_key, w_value, w_out, w_gate, w_up, w_down):
        mid_rows = attend_local(act_in, w_query, w_key, w_value, w_out, cp_size, tp_size)
        return dispatch_experts(mid_rows, route_ids, route_gates, w_gate, w_up, w_down, experts)

    return jax.shard_map(device_step, mesh=mesh, in_specs=(row_spec, row_spec, row_spec, head_spec, head_spec, head_spec, out_spec, expert_spec, expert_spec, expert_spec), out_specs=row_spec, check_vma=False)
```

profile of v0, /device:TPU:1, one launch (start us, length us, event | category | flops | bytes accessed | tf_op | source)
XLA Modules:
  0.0 449.3 jit_solution(13158231560091780165)
XLA Ops:
  7.3 16.9 %all-gather.4.cloned.1.call-done = bf16[2,128,2048]{2,1,0:T(8,128)(2,1)} async-done(((bf16[2,64,2048]{2,1,0:T(8,128)(2,1)}), bf16[2,128,2048]{2,1,0:T(8,128)(2,1)}) %all-gather.4.cloned.1.call-update) | async-done | bytes 1048592 | tf_op jit(solution)/shard_map/all_gather | solution.py:20
  24.2 2.6 convolution_convert_fusion
  28.7 2.6 convolution_convert_fusion.1
  31.4 7.1 %fusion.37 = bf16[2,128,16,128]{3,1,2,0:T(8,128)(2,1)} fusion(bf16[2048,16,128]{2,1,0:T(8,128)(2,1)} %param.13, bf16[2,128,2048]{2,1,0:T(8,128)(2,1)} %all-gather.4.cloned.1.call-done), kind=kOutput, calls=%fused_computation.38 | convolution fusion | flops 2148007936 | bytes 10485760 | tf_op jit(solution)/shard_map/bsh,hnd->bsnd/dot_general | solution.py:21
  38.5 68.0 %all-gather.8.cloned.1.call-done = bf16[2,8192,2,128]{3,1,2,0:T(8,128)(2,1)} async-done(((bf16[2,128,2,128]{3,1,2,0:T(8,128)(2,1)}), bf16[2,8192,2,128]{3,1,2,0:T(8,128)(2,1)}) %all-gather.8.cloned.1.call-update) | async-done | bytes 8388624 | tf_op jit(solution)/shard_map/all_gather | solution.py:25
  106.5 27.9 %fusion.4 = (f32[2,2,8,64]{3,2,1,0:T(8,128)S(1)}, f32[2,2,8192,64,8]{2,3,4,1,0:T(8,128)}) fusion(pred[64,8192]{1,0:T(8,128)(4,1)} %get-tuple-element.5, bf16[2,128,2,8,128]{4,1,3,2,0:T(8,128)(2,1)} %bitcast.162, bf16[2,8192,2,128]{3,1,2,0:T(8,128)(2,1)} %all-gather.8.cloned.1.call-done), kind=kOutput, calls=%fused_computation.11 | convolution fusion | flops 4345296896 | bytes 76554240 | tf_op jit(solution)/shard_map/bqhgd,bkhd->bhgqk/dot_general | solution.py:36
  134.4 22.7 %fusion = f32[2,2,8,64]{3,2,1,0:T(8,128)S(1)} fusion(f32[2,2,8192,64,8]{2,3,4,1,0:T(8,128)} %get-tuple-element.14, f32[2,2,8,64]{3,2,1,0:T(8,128)S(1)} %get-tuple-element.13, pred[64,8192]{1,0:T(8,128)(4,1)} %get-tuple-element.5), kind=kLoop, calls=%fused_computation.7 | loop fusion | flops 67106816 | bytes 67649536 | tf_op jit(solution)/shard_map/reduce_sum | solution.py:40
  157.1 27.8 %fusion.5 = (f32[2,2,8,64]{3,2,1,0:T(8,128)S(1)}, f32[2,2,8192,64,8]{2,3,4,1,0:T(8,128)}) fusion(pred[64,8192]{1,0:T(8,128)(4,1)} %get-tuple-element.6, bf16[2,128,2,8,128]{4,1,3,2,0:T(8,128)(2,1)} %bitcast.163, bf16[2,8192,2,128]{3,1,2,0:T(8,128)(2,1)} %all-gather.8.cloned.1.call-done), kind=kOutput, calls=%fused_computation.12 | convolution fusion | flops 4345296896 | bytes 76554240 | tf_op jit(solution)/shard_map/bqhgd,bkhd->bhgqk/dot_general | solution.py:36
  184.8 23.3 %fusion.2 = f32[2,2,8,64]{3,2,1,0:T(8,128)S(1)} fusion(f32[2,2,8192,64,8]{2,3,4,1,0:T(8,128)} %get-tuple-element.12, f32[2,2,8,64]{3,2,1,0:T(8,128)S(1)} %get-tuple-element.11, pred[64,8192]{1,0:T(8,128)(4,1)} %get-tuple-element.6), kind=kLoop, calls=%fused_computation.9 | loop fusion | flops 67106816 | bytes 67649536 | tf_op jit(solution)/shard_map/reduce_sum | solution.py:40
  208.2 27.5 %fusion.60 = bf16[2,64,2,8,128]{4,1,3,2,0:T(8,128)(2,1)} fusion(f32[2,2,8192,64,8]{2,3,4,1,0:T(8,128)} %get-tuple-element.14, f32[2,2,8,64]{3,2,1,0:T(8,128)S(1)} %get-tuple-element.13, pred[64,8192]{1,0:T(8,128)(4,1)} %get-tuple-element.5, bf16[2,8192,2,128]{3,1,2,0:T(8,128)(2,1)} %all-gather.6.cloned.1.call-done, f32[2,64,2,8]{1,3,2,0:T(8,128)S(1)} %bitcast.165), kind=kOutput, calls=%fused_computation.43 | convolution fusion | flops 4362600448 | bytes 76562432 | tf_op jit(solution)/shard_map/bhgqk,bkhd->bqhgd/dot_general | solution.py:41
  235.8 27.3 %fusion.65 = bf16[2,64,2,8,128]{4,1,3,2,0:T(8,128)(2,1)} fusion(f32[2,2,8192,64,8]{2,3,4,1,0:T(8,128)} %get-tuple-element.12, f32[2,2,8,64]{3,2,1,0:T(8,128)S(1)} %get-tuple-element.11, pred[64,8192]{1,0:T(8,128)(4,1)} %get-tuple-element.6, bf16[2,8192,2,128]{3,1,2,0:T(8,128)(2,1)} %all-gather.6.cloned.1.call-done, f32[2,64,2,8]{1,3,2,0:T(8,128)S(1)} %bitcast.166), kind=kOutput, calls=%fused_computation.44 | convolution fusion | flops 4362600448 | bytes 76562432 | tf_op jit(solution)/shard_map/bhgqk,bkhd->bqhgd/dot_general | solution.py:41
  264.3 6.2 %fusion.32 = f32[2,128,2048]{2,1,0:T(8,128)} fusion(bf16[2,128,16,128]{3,1,2,0:T(8,128)(2,1)S(1)} %bitcast.164, bf16[16,128,2048]{2,1,0:T(8,128)(2,1)} %param.16), kind=kOutput, calls=%fused_computation.36 | convolution fusion | flops 2147483648 | bytes 11534336 | tf_op jit(solution)/shard_map/bsnd,ndh->bsh/dot_general | solution.py:45
  271.6 12.5 %scatter_fusion = s32[2,256]{1,0:T(2,128)S(1)} fusion(s32[2,256]{1,0:T(2,128)S(1)} %broadcast_in_dim.73, s32[256]{0:T(256)S(1)} %get-tuple-element.10, s32[256]{0:T(256)S(1)} %broadcast_bitcast_fusion), kind=kCustom, calls=%fused_computation.2 | custom fusion | bytes 5120 | tf_op jit(solution)/shard_map/scatter | solution.py:59
  284.4 2.3 add_convert_fusion
  286.7 20.0 %gather_fusion = bf16[512,2048]{1,0:T(8,128)(2,1)} fusion(bf16[2,64,2048]{2,1,0:T(8,128)(2,1)} %add_convert_fusion, s32[512]{0:T(512)S(1)} %bitcast.161), kind=kCustom, calls=%fused_computation | custom fusion | bytes 4198400 | tf_op jit(solution)/shard_map/vmap(jit(_take))/gather | solution.py:8
  306.7 4.4 gather.13
  311.1 4.2 broadcast_select_fusion
  315.3 38.1 %all_to_all.10 = bf16[2,128,2,2048]{3,2,0,1:T(2,128)(2,1)S(1)} all-to-all(bf16[2,128,2,2048]{3,2,0,1:T(2,128)(2,1)S(1)} %broadcast_select_fusion), channel_id=1, replica_groups=mesh['data'=1,'cp'=64,'tp'=2] {'cp','tp'}, dimensions={1} | all-to-all | bytes 4194304 | tf_op jit(solution)/shard_map/all_to_all | solution.py:61
  353.3 2.7 copy.43
  356.1 4.1 reshape.152
  360.2 5.5 %fusion.27 = f32[2,256,768]{2,1,0:T(8,128)} fusion(bf16[2,256,2048]{2,1,0:T(8,128)(2,1)} %reshape.152, bf16[1,2048,768]{2,1,0:T(8,128)(2,1)} %param.17), kind=kOutput, calls=%fused_computation.33 | convolution fusion | flops 1610612736 | bytes 6815744 | tf_op jit(solution)/shard_map/bth,hf->btf/dot_general | solution.py:63
  365.7 8.2 %fusion.29 = bf16[2,256,2048]{2,1,0:T(8,128)(2,1)} fusion(bf16[1,768,2048]{2,1,0:T(8,128)(2,1)S(1)} %copy-done, f32[2,256,768]{2,1,0:T(8,128)} %fusion.27, bf16[2,256,2048]{2,1,0:T(8,128)(2,1)} %reshape.152, bf16[1,2048,768]{2,1,0:T(8,128)(2,1)} %param.18), kind=kOutput, calls=%fused_computation.35 | convolution fusion | flops 3224633344 | bytes 12058624 | tf_op jit(solution)/shard_map/btf,fh->bth/dot_general | solution.py:66
  373.9 4.4 reshape.153
  378.3 5.4 %copy.44 = bf16[2,128,2,2048]{3,2,0,1:T(2,128)(2,1)} copy(bf16[2,128,2,2048]{3,2,1,0:T(2,128)(2,1)} %reshape.153) | data formatting | bytes 4194304 | tf_op jit(solution)/shard_map/reshape | solution.py:67
  383.7 7.6 %all-to-all-start.1 = ((bf16[2,128,2,2048]{3,2,0,1:T(2,128)(2,1)}), bf16[2,128,2,2048]{3,2,0,1:T(2,128)(2,1)}, u32[]{:S(2)}, u32[]{:S(2)}) async-start(bf16[2,128,2,2048]{3,2,0,1:T(2,128)(2,1)} %copy.44), calls=%async_computation.2 | async-start | bytes 4194304 | tf_op jit(solution)/shard_map/all_to_all | solution.py:67
  391.6 30.8 %all-to-all-done.1 = bf16[2,128,2,2048]{3,2,0,1:T(2,128)(2,1)} async-done(((bf16[2,128,2,2048]{3,2,0,1:T(2,128)(2,1)}), bf16[2,128,2,2048]{3,2,0,1:T(2,128)(2,1)}, u32[]{:S(2)}, u32[]{:S(2)}) %all-to-all-start.1) | async-done | bytes 2097184 | tf_op jit(solution)/shard_map/all_to_all | solution.py:67
  422.4 4.3 copy.45
  426.7 4.1 reshape.154
  430.8 5.2 %gather_fusion.1 = bf16[256,2048]{1,0:T(8,128)(2,1)} fusion(bf16[2,256,2048]{2,1,0:T(8,128)(2,1)} %reshape.154, s32[256]{0:T(256)S(1)} %get-tuple-element.9), kind=kCustom, calls=%fused_computation.1 | custom fusion | bytes 2099200 | tf_op jit(solution)/shard_map/vmap(jit(_take))/gather | solution.py:8
  436.0 2.5 gather.15
  438.5 1.9 copy_select_fusion
  440.4 2.2 fusion.72
  (44 shorter events, 5.4 us)
Async XLA Ops:
  6.5 359.1 %copy-start = (bf16[1,768,2048]{2,1,0:T(8,128)(2,1)S(1)}, bf16[1,768,2048]{2,1,0:T(8,128)(2,1)}, u32[]{:S(2)}) copy-start(bf16[1,768,2048]{2,1,0:T(8,128)(2,1)} %param.19) | copy-start | bytes 9437188
  6.5 17.7 %all-gather.4.cloned.1.call-start = ((), (), s32[]{:S(2)}) async-start(), calls=%async_computation.3 | async-start | bytes 1572864 | tf_op jit(solution)/shard_map/all_gather | solution.py:20
  7.3 99.2 %all-gather.8.cloned.1.call-start = ((), (), s32[]{:S(2)}) async-start(), calls=%async_computation.5 | async-start | bytes 8519680 | tf_op jit(solution)/shard_map/all_gather | solution.py:25
  26.9 181.3 %all-gather.6.cloned.1.call-start = ((), (), s32[]{:S(2)}) async-start(), calls=%async_computation.4 | async-start | bytes 8519680 | tf_op jit(solution)/shard_map/all_gather | solution.py:26
  31.4 253.1 %reduce-scatter.2.cloned.1.call-start = ((), (), s32[]{:S(2)}) async-start(), calls=%async_computation.6 | async-start | bytes 3145728 | tf_op jit(solution)/shard_map/reduce_scatter | solution.py:46
  264.3 6.2 %copy-start.1 = (s32[2,64,2]{1,2,0:T(2,128)S(1)}, s32[2,64,2]{1,2,0:T(2,128)}, u32[]{:S(2)}) copy-start(s32[2,64,2]{1,2,0:T(2,128)} %param.11) | copy-start | bytes 3076
  373.9 17.7 %copy-start.2 = (f32[2,64,2]{1,2,0:T(2,128)S(1)}, f32[2,64,2]{1,2,0:T(2,128)}, u32[]{:S(2)}) copy-start(f32[2,64,2]{1,2,0:T(2,128)} %param.12) | copy-start | bytes 3076
  383.7 38.7 %all-to-all-start.1 = ((bf16[2,128,2,2048]{3,2,0,1:T(2,128)(2,1)}), bf16[2,128,2,2048]{3,2,0,1:T(2,128)(2,1)}, u32[]{:S(2)}, u32[]{:S(2)}) async-start(bf16[2,128,2,2048]{3,2,0,1:T(2,128)(2,1)} %copy.44), calls=%async_computation.2 | async-start | bytes 4194304 | tf_op jit(solution)/shard_map/all_to_all | solution.py:67
Sparse Core Ops, SparseCore 0:
  9.0 15.2 all-gather.3
  27.1 79.3 all-gather.7
  109.4 78.2 all-gather.5
  270.7 12.2 reduce-scatter.1
where the time goes:
time: 454 us; the launch traced here: 449 us
  matrix products  143 us (31%)
  waiting for transfers between devices  117 us (26%)
  local copies, waits for them, and re-layouts  70.6 us (16%)
  other arithmetic  60.1 us (13%)
  blocking collectives  38.1 us (8%)
  between operations  13.5 us (3%)
  starting transfers between devices  7.74 us (2%)
    all_gather x1, waiting for transfers between devices, attend_local(): key_all = lax.all_gather(key_half, 'cp', axis=1, tiled=True)  68 us
    dot_general x2, matrix products, attend_local(): jnp.einsum('bqhgd,bkhd->bhgqk', q_part, key_all, preferred_element_type=j...  55.6 us
    dot_general x2, matrix products, attend_local(): jnp.einsum('bhgqk,bkhd->bqhgd', exp_scores.astype(jnp.bfloat16), value_al...  54.8 us
    reduce_sum x2, other arithmetic, attend_local(): row_sum = jnp.sum(exp_scores, axis=-1)  46.1 us
    all_to_all x1, blocking collectives, dispatch_experts(): recv_buf = lax.all_to_all(send_buf, ('cp', 'tp'), 1, 1, tiled=True)  38.1 us
    gather x4, local copies, waits for them, and re-layouts, pick_rows(): return jnp.take(row_table, row_ids, axis=0, mode='fill', fill_value=0)  32.1 us
    all_to_all x1, waiting for transfers between devices, dispatch_experts(): lax.all_to_all(expert_out.reshape(n_micro, experts, capacity, hidden), ('...  30.8 us
    all_gather x1, waiting for transfers between devices, attend_local(): x_half = lax.all_gather(act_in, 'tp', axis=1, tiled=True)  16.9 us
  transfers between devices with their start and end apart: 5, of which 3 were waited for; matrix products, arithmetic and copies ran while one was open for 28% of the time, Pallas kernels for 0%

commit v1 on v0

v1 whole, which is shorter than its diff:
```python
import functools
import math

import jax
import jax.numpy as jnp
from jax import lax
from jax.experimental import pallas as pl
from jax.experimental.pallas import tpu as pltpu
from jax.sharding import PartitionSpec as P

F32 = jnp.float32
BF16 = jnp.bfloat16
HEAD = 128
GROUP = 8
PIECE = 64
TILE_PIECES = 8
TILE = TILE_PIECES * PIECE


def attn_kernel(cp_size, q_ref, k_ref, v_ref, o_ref, qs_ref, s_ref, mx_ref, l_ref, acc_ref):
    rank = lax.axis_index('cp')
    own_tile = rank // TILE_PIECES
    n_first = own_tile + 1
    half_tiles = cp_size // TILE_PIECES
    n_tiles = 2 * half_tiles + 1
    exp_scale = (HEAD ** -0.5) * math.log2(math.e)
    for piece in range(2):
        for g in range(GROUP):
            qs_ref[piece, g * PIECE:(g + 1) * PIECE, :] = q_ref[piece * PIECE:(piece + 1) * PIECE, g * HEAD:(g + 1) * HEAD]
    mx_ref[...] = jnp.full(mx_ref.shape, -jnp.inf, F32)
    l_ref[...] = jnp.zeros(l_ref.shape, F32)
    acc_ref[...] = jnp.zeros(acc_ref.shape, F32)
    row_in = lax.broadcasted_iota(jnp.int32, (TILE, 1), 0) % PIECE
    col = lax.broadcasted_iota(jnp.int32, (1, TILE), 1)

    def where_tile(i):
        is_first = i < n_first
        j = i - n_first
        lower = jnp.logical_or(is_first, j < half_tiles)
        half = jnp.where(lower, 0, 1)
        tile = jnp.where(is_first, i, jnp.where(lower, j, own_tile + j - half_tiles))
        return jnp.where(is_first, 0, 1), half, tile

    def key_slice(ref, half, tile):
        rows = ref[pl.ds(tile * TILE_PIECES, TILE_PIECES), pl.ds(pl.multiple_of(half * PIECE, PIECE), PIECE), :]
        return rows.reshape(TILE, HEAD)

    def score_step(i, carry):
        qi, half, tile = where_tile(i)
        s = lax.dot_general(qs_ref[qi], key_slice(k_ref, half, tile), (((1,), (1,)), ((), ())), preferred_element_type=F32)
        owner = tile * TILE_PIECES + col // PIECE
        key_piece = jnp.where(half == 0, owner, 2 * cp_size - 1 - owner)
        query_piece = jnp.where(qi == 0, rank, 2 * cp_size - 1 - rank)
        limit = (query_piece - key_piece) * PIECE - col % PIECE
        s = jnp.where(limit + row_in >= 0, s, -jnp.inf)
        s_ref[i] = s
        peak = mx_ref[qi]
        for b in range(TILE // HEAD):
            peak = jnp.maximum(peak, s[:, b * HEAD:(b + 1) * HEAD])
        mx_ref[qi] = peak
        return carry

    lax.fori_loop(0, n_tiles, score_step, 0)
    for piece in range(2):
        mx_ref[piece] = jnp.broadcast_to(jnp.max(mx_ref[piece], axis=1, keepdims=True), (TILE, HEAD))

    def value_step(i, carry):
        qi, half, tile = where_tile(i)
        peak = mx_ref[qi]
        total = l_ref[qi]
        blocks = []
        for b in range(TILE // HEAD):
            e = jnp.exp2((s_ref[i, :, b * HEAD:(b + 1) * HEAD] - peak) * exp_scale)
            total = total + e
            blocks.append(e.astype(BF16))
        l_ref[qi] = total
        e_tile = jnp.concatenate(blocks, axis=1)
        acc_ref[qi] += jnp.dot(e_tile, key_slice(v_ref, half, tile), preferred_element_type=F32)
        return carry

    lax.fori_loop(0, n_tiles, value_step, 0)
    for piece in range(2):
        out = (acc_ref[piece] / jnp.sum(l_ref[piece], axis=1, keepdims=True)).astype(BF16)
        for g in range(GROUP):
            o_ref[piece * PIECE:(piece + 1) * PIECE, g * HEAD:(g + 1) * HEAD] = out[g * PIECE:(g + 1) * PIECE, :]


def attention(q, kv, cp_size):
    kv3 = kv.reshape(cp_size, 2 * PIECE, kv.shape[-1])
    n_kv = kv.shape[-1] // HEAD // 2
    n_tiles = 2 * cp_size // TILE_PIECES + 1
    rows = 2 * PIECE
    return pl.pallas_call(
        functools.partial(attn_kernel, cp_size),
        out_shape=jax.ShapeDtypeStruct(q.shape, BF16),
        grid=(n_kv,),
        in_specs=[
            pl.BlockSpec((rows, GROUP * HEAD), lambda h: (0, h)),
            pl.BlockSpec((cp_size, rows, HEAD), lambda h: (0, 0, h)),
            pl.BlockSpec((cp_size, rows, HEAD), lambda h: (0, 0, n_kv + h)),
        ],
        out_specs=pl.BlockSpec((rows, GROUP * HEAD), lambda h: (0, h)),
        scratch_shapes=[
            pltpu.VMEM((2, TILE, HEAD), BF16),
            pltpu.VMEM((n_tiles, TILE, TILE), F32),
            pltpu.VMEM((2, TILE, HEAD), F32),
            pltpu.VMEM((2, TILE, HEAD), F32),
            pltpu.VMEM((2, TILE, HEAD), F32),
        ],
        compiler_params=pltpu.CompilerParams(vmem_limit_bytes=48 * 1024 * 1024),
        cost_estimate=pl.CostEstimate(flops=n_kv * n_tiles * TILE * TILE * HEAD * 4 * 2, bytes_accessed=kv.size * 2 + 2 * q.size * 2, transcendentals=n_kv * n_tiles * TILE * TILE),
        name='attention',
    )(q, kv3, kv3)


def solution(mesh):
    cp_size = mesh.shape['cp']
    tp_size = mesh.shape['tp']
    experts = cp_size * tp_size
    row_spec = P(None, ('data', 'cp', 'tp'), None)
    head_spec = P(None, 'tp', None)
    out_spec = P('tp', None, None)
    expert_spec = P(('cp', 'tp'), None, None)

    def device_step(act_in, route_ids, route_gates, w_query, w_key, w_value, w_out, w_gate, w_up, w_down):
        n_seq, tokens, hidden = act_in.shape
        x_half = lax.all_gather(act_in, 'tp', axis=1, tiled=True)
        kv_all = []
        for b in range(n_seq):
            k_half = jnp.einsum('sh,hnd->snd', x_half[b], w_key, preferred_element_type=F32).astype(BF16)
            v_half = jnp.einsum('sh,hnd->snd', x_half[b], w_value, preferred_element_type=F32).astype(BF16)
            kv = jnp.concatenate([k_half.reshape(2 * tokens, -1), v_half.reshape(2 * tokens, -1)], axis=1)
            kv_all.append(lax.all_gather(kv, 'cp', axis=0, tiled=True))
        q = jnp.einsum('bsh,hnd->bsnd', x_half, w_query, preferred_element_type=F32).astype(BF16)
        q = q.reshape(n_seq, 2 * tokens, -1)

        ids_chip = lax.all_gather(route_ids, 'tp', axis=0)
        flat = ids_chip.reshape(tp_size, n_seq, 2 * tokens)
        order = jnp.arange(2 * tokens)
        same = jnp.logical_and(flat[..., :, None] == flat[..., None, :], order[None, :] < order[:, None])
        slot = jnp.sum(same.astype(jnp.int32), axis=-1)
        part = (jnp.arange(tp_size)[:, None] * n_seq + jnp.arange(n_seq)[None, :])[..., None]
        row_of = (flat // tp_size) * (2 * tp_size * n_seq) + part * 2 + slot
        mine = flat % tp_size == lax.axis_index('tp')
        row_of = jnp.where(mine, row_of, -1).reshape(tp_size * n_seq * tokens, 2)
        slots = jnp.arange(cp_size * 2 * tp_size * n_seq, dtype=jnp.int32)
        pick0 = (row_of[:, 0:1] == slots[None, :])
        pick1 = (row_of[:, 1:2] == slots[None, :])
        send_pick = jnp.logical_or(pick0, pick1).astype(BF16)

        attn = [attention(q[b], kv_all[b], cp_size) for b in range(n_seq)]
        w_o = w_out.reshape(-1, hidden)
        partial = jnp.stack([jnp.dot(a, w_o, preferred_element_type=F32) for a in attn])
        attn_sum = lax.psum_scatter(partial, 'tp', scatter_dimension=1, tiled=True)
        h = (act_in.astype(F32) + attn_sum).astype(BF16)

        h_chip = lax.all_gather(h, 'tp', axis=0).reshape(tp_size * n_seq * tokens, hidden)
        send = lax.dot_general(send_pick, h_chip, (((0,), (0,)), ((), ())), preferred_element_type=F32).astype(BF16)
        recv = lax.all_to_all(send, 'cp', 0, 0, tiled=True)
        gate_act = jnp.dot(recv, w_gate[0], preferred_element_type=F32)
        up_act = jnp.dot(recv, w_up[0], preferred_element_type=F32)
        mixed = (jax.nn.silu(gate_act) * up_act).astype(BF16)
        z = jnp.dot(mixed, w_down[0], preferred_element_type=F32).astype(BF16)
        back = lax.all_to_all(z, 'cp', 0, 0, tiled=True)
        z0 = jnp.dot(pick0.astype(BF16), back, preferred_element_type=F32)
        z1 = jnp.dot(pick1.astype(BF16), back, preferred_element_type=F32)
        gates = lax.all_gather(route_gates, 'tp', axis=0).reshape(tp_size * n_seq * tokens, 2)
        mix = (gates[:, 0:1] * z0 + gates[:, 1:2] * z1).reshape(tp_size, n_seq, tokens, hidden)
        mix = lax.psum_scatter(mix, 'tp', scatter_dimension=0, tiled=False)
        return (h.astype(F32) + mix).astype(BF16)

    return jax.shard_map(device_step, mesh=mesh, in_specs=(row_spec, row_spec, row_spec, head_spec, head_spec, head_spec, out_spec, expert_spec, expert_spec, expert_spec), out_specs=row_spec, check_vma=False)
```

time: 454 us -> 373 us (0.82)
  matrix products: 143 us -> 43.2 us
  waiting for transfers between devices: 117 us -> 172 us
  other arithmetic: 60.1 us -> 7.74 us
  Pallas kernels: 0 us -> 49.9 us
  local copies, waits for them, and re-layouts: 70.6 us -> 30 us
  blocking collectives: 38.1 us -> 45.4 us
    dot_general x10 -> x8, matrix products: 143 us -> 35.9 us  [the longest x2 10.4 us: device_step(): jnp.dot(a, w_o, preferred_element_type=F32)]
    pallas_call x0 -> x2, Pallas kernels: none -> 49.9 us  [attention(): pl.pallas_call(functools.partial(attn_kernel, cp_size), out_shape=jax.Sha...]
    reduce_sum x3 -> x1, other arithmetic: 46.2 us -> 0.25 us  [device_step(): slot = jnp.sum(same.astype(jnp.int32), axis=-1)]
    all_gather x3 -> x4, waiting for transfers between devices: 85 us -> 118 us  [the longest x2 99.3 us: device_step(): kv_all.append(lax.all_gather(kv, 'cp', axis=0, tiled=True))]
    gather x4 -> x0, local copies, waits for them, and re-layouts: 32.1 us -> none  [pick_rows(): return jnp.take(row_table, row_ids, axis=0, mode='fill', fill_value=0)]
    unnamed x8 -> x19, local copies, waits for them, and re-layouts: 0.12 us -> 23.5 us
    reduce_scatter x1 -> x2, waiting for transfers between devices: 0.02 us -> 20.8 us  [the longest x1 12.4 us: device_step(): attn_sum = lax.psum_scatter(partial, 'tp', scatter_dimension=1, tiled=True)]
    reshape x5 -> x6, local copies, waits for them, and re-layouts: 18.2 us -> 0.59 us  [the longest x2 0.21 us: device_step(): v_half.reshape(2 * tokens, -1)]
  transfers between devices with their start and end apart: 5 -> 7, of which waited for: 3 -> 7; matrix products, arithmetic and copies ran while one was open for 28% -> 12% of each run, Pallas kernels for 0% -> 7%
where the time goes in v1:
time: 373 us; the launch traced here: 371 us
  waiting for transfers between devices  172 us (46%)
  Pallas kernels  49.9 us (13%)
  blocking collectives  45.4 us (12%)
  matrix products  43.2 us (12%)
  local copies, waits for them, and re-layouts  30 us (8%)
  between operations  13.7 us (4%)
  starting transfers between devices  9.92 us (3%)
  other arithmetic  7.74 us (2%)
    all_gather x2, waiting for transfers between devices, device_step(): kv_all.append(lax.all_gather(kv, 'cp', axis=0, tiled=True))  99.3 us
    pallas_call x2, Pallas kernels, attention(): pl.pallas_call(functools.partial(attn_kernel, cp_size), out_shape=jax.Sha...  49.9 us
    all_to_all x1, blocking collectives, device_step(): recv = lax.all_to_all(send, 'cp', 0, 0, tiled=True)  41.3 us
    all_to_all x1, waiting for transfers between devices, device_step(): back = lax.all_to_all(z, 'cp', 0, 0, tiled=True)  31.6 us
    unnamed x19, local copies, waits for them, and re-layouts  23.5 us
    reduce_scatter x1, waiting for transfers between devices, device_step(): attn_sum = lax.psum_scatter(partial, 'tp', scatter_dimension=1, tiled=True)  12.4 us
    dot_general x2, matrix products, device_step(): jnp.dot(a, w_o, preferred_element_type=F32)  10.4 us
    all_gather x1, waiting for transfers between devices, device_step(): lax.all_gather(h, 'tp', axis=0).reshape(tp_size * n_seq * tokens, hidden)  9.73 us
  transfers between devices with their start and end apart: 7, of which 7 were waited for; matrix products, arithmetic and copies ran while one was open for 12% of the time, Pallas kernels for 7%

profile of v1, /device:TPU:1, one launch (start us, length us, event | category | flops | bytes accessed | tf_op | source)
XLA Modules:
  0.0 371.5 jit_solution(4953824809809591402)
XLA Ops:
  7.3 3.9 %copy.57 = bf16[2048,2,128]{0,2,1:T(8,128)(2,1)} copy(bf16[2048,2,128]{2,1,0:T(2,128)(2,1)} %param.15) | data formatting | bytes 2097152 | tf_op args[5]
  11.2 3.8 %copy.56 = bf16[2048,2,128]{0,2,1:T(8,128)(2,1)} copy(bf16[2048,2,128]{2,1,0:T(2,128)(2,1)} %param.14) | data formatting | bytes 2097152 | tf_op args[4]
  14.9 9.3 %all-gather.8.cloned.1.call-done = bf16[2,128,2048]{2,1,0:T(8,128)(2,1)} async-done(((bf16[2,64,2048]{2,1,0:T(8,128)(2,1)}), bf16[2,128,2048]{2,1,0:T(8,128)(2,1)}) %all-gather.8.cloned.1.call-update) | async-done | bytes 1048592 | tf_op jit(solution)/shard_map/all_gather | solution.py:127
  24.2 1.8 fusion.38
  26.2 1.8 fusion.39
  28.9 1.8 fusion.36
  30.9 1.8 fusion.37
  33.6 12.4 %copy.54 = bf16[2048,16,128]{0,2,1:T(8,128)(2,1)} copy(bf16[2048,16,128]{2,1,0:T(8,128)(2,1)} %param.13) | data formatting | bytes 16777216 | tf_op args[3]
  46.0 6.1 %fusion.24 = bf16[2,128,16,128]{1,3,2,0:T(8,128)(2,1)S(1)} fusion(bf16[2048,16,128]{0,2,1:T(8,128)(2,1)} %copy.54, bf16[2,128,2048]{2,1,0:T(8,128)(2,1)} %all-gather.8.cloned.1.call-done), kind=kOutput, calls=%fused_computation.23 | convolution fusion | flops 2148007936 | bytes 10485760 | tf_op jit(solution)/shard_map/bsh,hnd->bsnd/dot_general | solution.py:134
  53.2 2.0 copy.72.q_ref
  55.2 2.1 copy.71.q_ref
  57.3 50.4 %all-gather.12.cloned.1.call-done = bf16[8192,512]{1,0:T(8,128)(2,1)} async-done(((bf16[128,512]{1,0:T(8,128)(2,1)}), bf16[8192,512]{1,0:T(8,128)(2,1)}) %all-gather.12.cloned.1.call-update) | async-done | bytes 8388624 | tf_op jit(solution)/shard_map/all_gather | solution.py:133
  108.8 25.0 %attention.3 = bf16[128,2048]{1,0:T(8,128)(2,1)S(1)} custom-call(bf16[128,2048]{1,0:T(8,128)(2,1)S(1)} %copy-done.2, bf16[64,128,512]{2,1,0:T(8,128)(2,1)} %bitcast.121, bf16[64,128,512]{2,1,0:T(8,128)(2,1)} %bitcast.122), custom_call_target="tpu_custom_call" | custom-call | flops 9126805504 | bytes 9437184 | tf_op jit(solution)/shard_map/attention/pallas_call | solution.py:93
  133.7 5.7 %convolution_bitcast_fusion = f32[1,128,2048]{2,1,0:T(8,128)} fusion(bf16[128,2048]{1,0:T(8,128)(2,1)S(1)} %attention.3, bf16[2048,2048]{1,0:T(8,128)(2,1)} %bitcast.97), kind=kOutput, calls=%fused_computation.15 | convolution fusion | flops 1073741824 | bytes 9961472 | tf_op jit(solution)/shard_map/dot_general | solution.py:153
  139.4 48.8 %all-gather.10.cloned.1.call-done = bf16[8192,512]{1,0:T(8,128)(2,1)} async-done(((bf16[128,512]{1,0:T(8,128)(2,1)}), bf16[8192,512]{1,0:T(8,128)(2,1)}) %all-gather.10.cloned.1.call-update) | async-done | bytes 8388624 | tf_op jit(solution)/shard_map/all_gather | solution.py:133
  189.3 25.0 %attention.2 = bf16[128,2048]{1,0:T(8,128)(2,1)S(1)} custom-call(bf16[128,2048]{1,0:T(8,128)(2,1)S(1)} %copy-done.1, bf16[64,128,512]{2,1,0:T(8,128)(2,1)} %bitcast.123, bf16[64,128,512]{2,1,0:T(8,128)(2,1)} %bitcast.124), custom_call_target="tpu_custom_call" | custom-call | flops 9126805504 | bytes 9437184 | tf_op jit(solution)/shard_map/attention/pallas_call | solution.py:93
  214.3 4.7 %convolution_bitcast_fusion.1 = f32[1,128,2048]{2,1,0:T(8,128)S(1)} fusion(bf16[128,2048]{1,0:T(8,128)(2,1)S(1)} %attention.2, bf16[2048,2048]{1,0:T(8,128)(2,1)} %bitcast.98), kind=kOutput, calls=%fused_computation.16 | convolution fusion | flops 1073741824 | bytes 9961472 | tf_op jit(solution)/shard_map/dot_general | solution.py:153
  220.6 12.4 %reduce-scatter.3.cloned.1.call-done = f32[2,64,2048]{2,1,0:T(8,128)} async-done(((f32[2,128,2048]{2,1,0:T(8,128)}), f32[2,64,2048]{2,1,0:T(8,128)}) %reduce-scatter.3.cloned.1.call-update) | async-done | bytes 1048592 | tf_op jit(solution)/shard_map/reduce_scatter | solution.py:154
  232.9 2.3 add_convert_fusion
  235.2 2.0 all-gather.1
  238.5 9.7 %all-gather.14.cloned.1.call-done = bf16[4,64,2048]{2,1,0:T(8,128)(2,1)} async-done(((bf16[2,64,2048]{2,1,0:T(8,128)(2,1)}), bf16[4,64,2048]{2,1,0:T(8,128)(2,1)}) %all-gather.14.cloned.1.call-update) | async-done | bytes 1048592 | tf_op jit(solution)/shard_map/all_gather | solution.py:157
  248.2 2.1 fusion.11
  250.3 41.3 %all_to_all.24 = bf16[64,8,2048]{2,1,0:T(8,128)(2,1)S(1)} all-to-all(bf16[64,8,2048]{2,1,0:T(8,128)(2,1)S(1)} %fusion.11), channel_id=1, replica_groups=mesh['data'=1,'cp'=64,'tp'=2] {'cp'}, dimensions={0} | all-to-all | bytes 4194304 | tf_op jit(solution)/shard_map/all_to_all | solution.py:159
  292.9 3.0 fusion.6
  295.9 8.3 %fusion.12 = bf16[64,8,2048]{2,1,0:T(8,128)(2,1)} fusion(bf16[1,768,2048]{2,1,0:T(8,128)(2,1)S(1)} %copy-done, f32[512,768]{1,0:T(8,128)} %fusion.6, bf16[1,2048,768]{2,1,0:T(8,128)(2,1)} %param.18, bf16[64,8,2048]{2,1,0:T(8,128)(2,1)} %copy-done.4), kind=kOutput, calls=%fused_computation.11 | convolution fusion | flops 3224633344 | bytes 12058624 | tf_op jit(solution)/shard_map/dot_general | solution.py:163
  304.2 9.7 %all-to-all-start.1 = ((bf16[64,8,2048]{2,1,0:T(8,128)(2,1)}), bf16[64,8,2048]{2,1,0:T(8,128)(2,1)}, u32[]{:S(2)}, u32[]{:S(2)}) async-start(bf16[64,8,2048]{2,1,0:T(8,128)(2,1)} %fusion.12), calls=%async_computation.2 | async-start | bytes 4194304 | tf_op jit(solution)/shard_map/all_to_all | solution.py:164
  314.0 2.1 all-gather
  316.2 31.6 %all-to-all-done.1 = bf16[64,8,2048]{2,1,0:T(8,128)(2,1)} async-done(((bf16[64,8,2048]{2,1,0:T(8,128)(2,1)}), bf16[64,8,2048]{2,1,0:T(8,128)(2,1)}, u32[]{:S(2)}, u32[]{:S(2)}) %all-to-all-start.1) | async-done | bytes 2097184 | tf_op jit(solution)/shard_map/all_to_all | solution.py:164
  347.8 2.3 convolution_multiply_fusion.1
  350.2 3.7 %fusion.15 = f32[256,2048]{1,0:T(8,128)} fusion(f32[256,2048]{1,0:T(8,128)S(1)} %convolution_multiply_fusion.1, bf16[64,8,2048]{2,1,0:T(8,128)(2,1)} %all-to-all-done.1, f32[256]{0:T(256)S(1)} %bitcast.119, s32[256]{0:T(256)S(1)} %bitcast.116), kind=kOutput, calls=%fused_computation.13 | convolution fusion | flops 538050560 | bytes 6293504 | tf_op jit(solution)/shard_map/dot_general | solution.py:166
  354.0 8.4 %reduce-scatter.5.cloned.1.call-done = f32[1,2,64,2048]{3,2,1,0:T(8,128)} async-done(((f32[2,2,64,2048]{3,2,1,0:T(8,128)}), f32[1,2,64,2048]{3,2,1,0:T(8,128)}) %reduce-scatter.5.cloned.1.call-update) | async-done | bytes 1048592 | tf_op jit(solution)/shard_map/reduce_scatter | solution.py:169
  362.4 2.3 fusion.28
  (58 shorter events, 10.1 us)
Async XLA Ops:
  6.5 289.4 %copy-start = (bf16[1,768,2048]{2,1,0:T(8,128)(2,1)S(1)}, bf16[1,768,2048]{2,1,0:T(8,128)(2,1)}, u32[]{:S(2)}) copy-start(bf16[1,768,2048]{2,1,0:T(8,128)(2,1)} %param.19) | copy-start | bytes 9437188
  6.5 17.7 %all-gather.8.cloned.1.call-start = ((), (), s32[]{:S(2)}) async-start(), calls=%async_computation.4 | async-start | bytes 1572864 | tf_op jit(solution)/shard_map/all_gather | solution.py:127
  7.3 100.5 %all-gather.12.cloned.1.call-start = ((), (), s32[]{:S(2)}) async-start(), calls=%async_computation.6 | async-start | bytes 8519680 | tf_op jit(solution)/shard_map/all_gather | solution.py:133
  28.9 159.4 %all-gather.10.cloned.1.call-start = ((), (), s32[]{:S(2)}) async-start(), calls=%async_computation.5 | async-start | bytes 8519680 | tf_op jit(solution)/shard_map/all_gather | solution.py:133
  33.5 199.4 %reduce-scatter.3.cloned.1.call-start = ((), (), s32[]{:S(2)}) async-start(), calls=%async_computation.7 | async-start | bytes 3145728 | tf_op jit(solution)/shard_map/reduce_scatter | solution.py:154
  107.7 1.0 copy-start.2
  188.3 1.0 copy-start.1
  214.3 4.7 %copy-start.3 = (f32[1,128,2048]{2,1,0:T(8,128)S(1)}, f32[1,128,2048]{2,1,0:T(8,128)}, u32[]{:S(2)}) copy-start(f32[1,128,2048]{2,1,0:T(8,128)} %convolution_bitcast_fusion) | copy-start | bytes 3145732
  220.5 14.7 %copy-start.5 = (s32[2,64,2]{1,2,0:T(2,128)S(1)}, s32[2,64,2]{1,2,0:T(2,128)}, u32[]{:S(2)}) copy-start(s32[2,64,2]{1,2,0:T(2,128)} %param.11) | copy-start | bytes 3076
  220.5 27.7 %all-gather.14.cloned.1.call-start = ((), (), s32[]{:S(2)}) async-start(), calls=%async_computation.9 | async-start | bytes 1572864 | tf_op jit(solution)/shard_map/all_gather | solution.py:157
  250.3 42.6 %copy-start.7 = (bf16[1,2048,768]{2,1,0:T(8,128)(2,1)S(1)}, bf16[1,2048,768]{2,1,0:T(8,128)(2,1)}, u32[]{:S(2)}) copy-start(bf16[1,2048,768]{2,1,0:T(8,128)(2,1)} %param.17) | copy-start | bytes 9437188
  291.6 1.3 copy-start.4
  304.2 9.8 %copy-start.6 = (f32[2,64,2]{1,2,0:T(2,128)S(1)}, f32[2,64,2]{1,2,0:T(2,128)}, u32[]{:S(2)}) copy-start(f32[2,64,2]{1,2,0:T(2,128)} %param.12) | copy-start | bytes 3076
  304.2 43.6 %all-to-all-start.1 = ((bf16[64,8,2048]{2,1,0:T(8,128)(2,1)}), bf16[64,8,2048]{2,1,0:T(8,128)(2,1)}, u32[]{:S(2)}, u32[]{:S(2)}) async-start(bf16[64,8,2048]{2,1,0:T(8,128)(2,1)} %fusion.12), calls=%async_computation.2 | async-start | bytes 4194304 | tf_op jit(solution)/shard_map/all_to_all | solution.py:164
  313.9 48.5 %reduce-scatter.5.cloned.1.call-start = ((), (), s32[]{:S(2)}) async-start(), calls=%async_computation.8 | async-start | bytes 3145728 | tf_op jit(solution)/shard_map/reduce_scatter | solution.py:169
Sparse Core Ops, SparseCore 0:
  9.0 15.2 all-gather.7
  29.0 78.6 all-gather.11
  110.6 77.6 all-gather.9
  220.6 12.2 reduce-scatter.2
  235.3 12.8 all-gather.13
  354.1 8.2 reduce-scatter.4
